TPU v7x, 32 devices: a whole 2x2x4 slice. The times are simulated.
32 devices in a mesh: lat: 4 (over y, core), lon: 8 (over z, x).
Axes of the slice: x: 2, y: 2, z: 4, core: 2. Of those that a mesh axis runs over, the one named last changes fastest.
Arguments:
- layer_temp: float32 [64, 35, 1024], P('lat', None, 'lon'), may hold values from -20 to -2
- ice_depth_per_class: float32 [64, 5, 1024], P('lat', None, 'lon'), may hold values from 0.5 to 3
- ice_area: float32 [64, 5, 1024], P('lat', None, 'lon'), may hold values from 0.05 to 0.2
- surf_temp: float32 [64, 1024], P('lat', 'lon'), may hold values from -30 to -2
- seawater_thermal_input: float32 [64, 1024], P('lat', 'lon'), may hold values from 0 to 0.3
- velocity: float32 [2, 64, 1024], P(None, 'lat', 'lon'), may hold values from -1.2 to 1.2
- stress: float32 [3, 64, 1024], P(None, 'lat', 'lon'), may hold values from -3 to 3
- wind_stress: float32 [2, 64, 1024], P(None, 'lat', 'lon'), may hold values from -1.8 to 1.8
- current: float32 [2, 64, 1024], P(None, 'lat', 'lon'), may hold values from -1.8 to 1.8
- land_mask: int32 [64, 1024], P('lat', 'lon'), may hold values 0 or 1
- ice_mask: int32 [8, 64], P('lon', 'lat'), may hold values from 0 to 1, as said below
- band_index: int32 [64], P('lat'), may hold values from 0 to 15, as said below
Outputs:
- temp_after: float32 [64, 35, 1024], P('lat', None, 'lon')
- thick_after: float32 [64, 5, 1024], P('lat', None, 'lon')
- velocity_after: float32 [2, 64, 1024], P(None, 'lat', 'lon')
- stress_after: float32 [3, 64, 1024], P(None, 'lat', 'lon')
- zonal_volume: float32 [16], P('lat')
Inputs may be any that keep to these rules, and one draw needn't show every extreme that they name: `ice_mask`: for each lat index, the strips of all devices with that index include at most 56 ice-covered strips and more than (6) times the number of lon devices; among these devices one has all its 16 strips ice-covered. `band_index`: every band holds 1 to 7 rows, which lie next to one another; one band holds exactly 7.
All inputs are finite; a program needn't handle non-finite values. No bound on the sum of `land_mask` on one device may be relied on, other than what follows from the above.
Results may differ from a plain program's by a relative error of at most 0.00002.
Values sent between devices are 32-bit elements; how exact they have to be, the bound alone decides.
A program may use at most 64 MiB of HBM per device.

v0:
```python
import jax
import jax.numpy as jnp
from jax import lax
from jax.sharding import PartitionSpec as P

DEPTH_CLASSES = 5
VERTICAL_LEVELS = 7
SUBCYCLES = 3
SWEEPS = 2
BANDS_DEV = 4


FREEZE_POINT = -1.8
BASE_CONDUCT = 2.03
SALT_CONDUCT = 0.416
CONDUCT_SCALE = 1.0
GROWTH_RATE = 0.02
STRENGTH_SCALE = 1.0
STRENGTH_DECAY = 5.0
ELLIPSE_SQUARE = 4.0
STRAIN_FLOOR = 0.0025
STRESS_RELAX = 0.5
MOMENTUM_STEP = 0.5
WATER_DRAG = 1.0


def with_halo(value, sides, width):
    for axis, dim in sides:
        size, length = (lax.axis_size(axis), value.shape[dim])
        up = [(i, (i + 1) % size) for i in range(size)]
        down = [(j, i) for i, j in up]
        last = lax.slice_in_dim(value, length - width, length, axis=dim)
        leading = lax.slice_in_dim(value, 0, width, axis=dim)
        before = lax.ppermute(last, axis, up)
        after = lax.ppermute(leading, axis, down)
        value = jnp.concatenate([before, value, after], axis=dim)
    return value


def update_vertical_cell(
    thermal_state_levels, ice_depth_per_class, upper_interface_state, seawater_thermal_input
):
    first_extent = thermal_state_levels.shape[:-2]
    vertical_cell_group = thermal_state_levels.shape[-1]
    vertical_levels_state = thermal_state_levels.reshape(
        first_extent + (DEPTH_CLASSES, VERTICAL_LEVELS, vertical_cell_group)
    )
    before = [vertical_levels_state[..., layer_at, :] for layer_at in range(VERTICAL_LEVELS)]
    surface_row = upper_interface_state[..., None, :]
    scaled = CONDUCT_SCALE / (ice_depth_per_class * ice_depth_per_class)
    repeated_pass = before
    for picard_turn in range(SWEEPS):
        conductance = [BASE_CONDUCT + SALT_CONDUCT / guessed for guessed in repeated_pass]
        couplings = [scaled * conductance[0]]
        for layer_at in range(1, VERTICAL_LEVELS):
            couplings.append(scaled * 0.5 * (conductance[layer_at - 1] + conductance[layer_at]))
        couplings.append(scaled * conductance[VERTICAL_LEVELS - 1])
        upper_ratio = []
        eliminated = []
        for layer_at in range(VERTICAL_LEVELS):
            source_term = before[layer_at]
            divisor = 1.0 + couplings[layer_at] + couplings[layer_at + 1]
            if layer_at == 0:
                source_term = source_term + couplings[0] * surface_row
            else:
                divisor = divisor - couplings[layer_at] * upper_ratio[layer_at - 1]
                source_term = source_term + couplings[layer_at] * eliminated[layer_at - 1]
            if layer_at == VERTICAL_LEVELS - 1:
                source_term = source_term + couplings[VERTICAL_LEVELS] * FREEZE_POINT
            upper_ratio.append(couplings[layer_at + 1] / divisor)
            eliminated.append(source_term / divisor)
        solved = list(eliminated)
        for layer_at in range(VERTICAL_LEVELS - 2, -1, -1):
            solved[layer_at] = eliminated[layer_at] + upper_ratio[layer_at] * solved[layer_at + 1]
        repeated_pass = solved
    bottom = repeated_pass[VERTICAL_LEVELS - 1]
    regrown = (
        ice_depth_per_class
        + GROWTH_RATE
        * (BASE_CONDUCT + SALT_CONDUCT / bottom)
        * (FREEZE_POINT - bottom)
        / ice_depth_per_class
        - seawater_thermal_input[..., None, :]
    )
    updated_vertical_cells = jnp.stack(repeated_pass, axis=-2).reshape(thermal_state_levels.shape)
    return (updated_vertical_cells, regrown)


def stress_update(zonal_field, meridional_field, previous, strength):
    zonal_east = (zonal_field[1:-1, 2:] - zonal_field[1:-1, :-2]) * 0.5
    zonal_north = (zonal_field[2:, 1:-1] - zonal_field[:-2, 1:-1]) * 0.5
    meridional_east = (meridional_field[1:-1, 2:] - meridional_field[1:-1, :-2]) * 0.5
    meridional_north = (meridional_field[2:, 1:-1] - meridional_field[:-2, 1:-1]) * 0.5
    divergence = zonal_east + meridional_north
    tension = zonal_east - meridional_north
    shearing = zonal_north + meridional_east
    deformation = jnp.sqrt(
        divergence * divergence
        + (tension * tension + shearing * shearing) / ELLIPSE_SQUARE
        + STRAIN_FLOOR
    )
    viscous = strength / deformation
    bulk_new = (previous[0] + STRESS_RELAX * viscous * (divergence - deformation)) / (
        1.0 + STRESS_RELAX
    )
    tension_new = (previous[1] + STRESS_RELAX * viscous * tension / ELLIPSE_SQUARE) / (
        1.0 + STRESS_RELAX
    )
    shear_new = (previous[2] + STRESS_RELAX * viscous * shearing / (2.0 * ELLIPSE_SQUARE)) / (
        1.0 + STRESS_RELAX
    )
    return jnp.stack([bulk_new, tension_new, shear_new])


def force_update(padded, velocity, ice_mass, wind_stress, current, wet_cells):
    normal_east = 0.5 * (padded[0] + padded[1])
    normal_north = 0.5 * (padded[0] - padded[1])
    shear_stress = padded[2]
    push_east = (normal_east[1:-1, 2:] - normal_east[1:-1, :-2]) * 0.5 + (
        shear_stress[2:, 1:-1] - shear_stress[:-2, 1:-1]
    ) * 0.5
    push_north = (shear_stress[1:-1, 2:] - shear_stress[1:-1, :-2]) * 0.5 + (
        normal_north[2:, 1:-1] - normal_north[:-2, 1:-1]
    ) * 0.5
    pushes = jnp.stack([push_east, push_north])
    moved = velocity + MOMENTUM_STEP * (pushes / ice_mass + wind_stress + WATER_DRAG * current)
    return wet_cells * moved / (1.0 + MOMENTUM_STEP * WATER_DRAG)


def local(
    layer_temp,
    ice_depth_per_class,
    ice_area,
    surf_temp,
    seawater_thermal_input,
    velocity,
    stress,
    wind_stress,
    current,
    land_mask,
    ice_mask,
    band_index,
):
    rows_here = layer_temp.shape[0]
    cols_here = layer_temp.shape[2]
    lat_here = lax.axis_index("lat")
    lat_size = lax.axis_size("lat")
    volume_start = jnp.sum(ice_area * ice_depth_per_class, axis=1)
    coverage = jnp.sum(ice_area, axis=1)
    strength = STRENGTH_SCALE * volume_start * jnp.exp(-STRENGTH_DECAY * (1.0 - coverage))
    ice_mass = 1.0 + volume_start
    wet_cells = land_mask.astype(jnp.float32)
    row_ids = jnp.arange(rows_here + 4)
    outside = (lat_here == 0) & (row_ids < 2) | (lat_here == lat_size - 1) & (
        row_ids >= rows_here + 2
    )
    moving = velocity
    stresses = stress
    for subcycle in range(SUBCYCLES):
        stacked = jnp.concatenate([moving, stresses, strength[None]], axis=0)
        widened = with_halo(stacked, (("lat", 1), ("lon", 2)), 2)
        widened = jnp.where(outside[None, :, None], 0.0, widened)
        margin_stress = stress_update(
            widened[0], widened[1], widened[2:5, 1:-1, 1:-1], widened[5, 1:-1, 1:-1]
        )
        moving = force_update(margin_stress, moving, ice_mass, wind_stress, current, wet_cells)
        stresses = margin_stress[:, 1:-1, 1:-1]
    ice_rows = ice_mask[0]
    stepped_temp, stepped_thick = update_vertical_cell(
        layer_temp, ice_depth_per_class, surf_temp, seawater_thermal_input
    )
    strip_ice = (ice_rows == 1)[:, None, None]
    temp_after = jnp.where(strip_ice, stepped_temp, layer_temp)
    thick_after = jnp.where(strip_ice, stepped_thick, ice_depth_per_class)
    volume_after = jnp.sum(ice_area * thick_after, axis=1)
    row_total = jnp.sum(volume_after, axis=1)
    band_count = BANDS_DEV * lat_size
    members = (band_index[:, None] == jnp.arange(band_count, dtype=jnp.int32)[None, :]).astype(
        jnp.float32
    )
    part_sum = jnp.sum(members * row_total[:, None], axis=0)
    part_cells = jnp.sum(members, axis=0) * cols_here
    whole_sum, whole_cells = lax.psum((part_sum, part_cells), ("lat", "lon"))
    start = lat_here * BANDS_DEV
    share_sum = lax.dynamic_slice_in_dim(whole_sum, start, BANDS_DEV)
    share_cells = lax.dynamic_slice_in_dim(whole_cells, start, BANDS_DEV)
    zonal_volume = share_sum / share_cells
    return (temp_after, thick_after, moving, stresses, zonal_volume)


def solution(mesh):
    return jax.shard_map(
        local,
        mesh=mesh,
        in_specs=(
            P("lat", None, "lon"),
            P("lat", None, "lon"),
            P("lat", None, "lon"),
            P("lat", "lon"),
            P("lat", "lon"),
            P(None, "lat", "lon"),
            P(None, "lat", "lon"),
            P(None, "lat", "lon"),
            P(None, "lat", "lon"),
            P("lat", "lon"),
            P("lon", "lat"),
            P("lat"),
        ),
        out_specs=(
            P("lat", None, "lon"),
            P("lat", None, "lon"),
            P(None, "lat", "lon"),
            P(None, "lat", "lon"),
            P("lat"),
        ),
        check_vma=False,
    )
```

profile of v0, /device:TPU:0, one launch (start us, length us, event | category | flops | bytes accessed | tf_op | source)
XLA Modules:
  0.0 85.0 jit_solution(7143305279351373648)
XLA Ops:
  0.6 0.7 compare_bitcast_fusion
  1.3 1.1 %add_divide_fusion.6 = (f32[16,5,128]{2,0,1:T(8,128)S(1)}, f32[16,5,128]{2,0,1:T(8,128)S(1)}, f32[16,5,128]{2,0,1:T(8,128)S(1)}, f32[16,5,128]{2,0,1:T(8,128)S(1...) fusion(f32[16,5,7,128]{3,0,2,1:T(8,128)} %bitcast.328, ...), kind=kLoop, calls=%fused_computation.92 | loop fusion | flops 768000 | bytes 786432 | tf_op jit(solution)/shard_map/div | solution.py:71
  2.6 0.7 copy-done.7
  3.3 1.0 %multiply_reduce_fusion = (f32[16]{0:T(128)S(1)}, f32[16,128]{1,0:T(8,128)S(1)}, f32[16,128]{1,0:T(8,128)S(1)}, f32[16,5,128]{2,0,1:T(8,128)}, f32[16,5,128]{2,0...) fusion(f32[16,5,128]{2,0,1:T(8,128)S(1)} %copy-done.7, ...), kind=kLoop, calls=%fused_computation.48 | loop fusion | flops 1316848 | bytes 1261648 | tf_op jit(solution)/shard_map/reduce_sum | solution.py:176
  4.3 0.7 copy-done.2
  5.0 2.5 %collective-permute-start.1 = (f32[6,2,128]{2,1,0:T(2,128)S(1)}, f32[6,2,128]{2,1,0:T(2,128)S(1)}, u32[]{:S(2)}, u32[]{:S(2)}) collective-permute-start(f32[6,2,128]{2,1,0:T(2,128)S(1)} %get-tuple-element.78), channel_id=1, source_target_pairs={{8,0},{16,8},{24,16},{0,24},{9,1},{17,9},{25,17},{1,25},{10,2},{18... | collective-permute-start | bytes 18440 | tf_op jit(solution)/shard_map/ppermute | solution.py:35
  7.8 1.1 %collective-permute-done.1 = f32[6,2,128]{2,1,0:T(2,128)S(1)} collective-permute-done((f32[6,2,128]{2,1,0:T(2,128)S(1)}, f32[6,2,128]{2,1,0:T(2,128)S(1)}, u32[]{:S(2)}, u32[]{:S(2)}) %collective-permute-start.1) | collective-permute-done | bytes 6176 | tf_op jit(solution)/shard_map/ppermute | solution.py:35
  8.8 1.7 %collective-permute-done = f32[6,2,128]{2,1,0:T(2,128)S(1)} collective-permute-done((f32[6,2,128]{2,1,0:T(2,128)S(1)}, f32[6,2,128]{2,1,0:T(2,128)S(1)}, u32[]{:S(2)}, u32[]{:S(2)}) %collective-permute-start) | collective-permute-done | bytes 6176 | tf_op jit(solution)/shard_map/ppermute | solution.py:34
  10.6 4.6 %collective-permute-start.3 = (f32[6,20,2]{2,1,0:T(8,128)S(1)}, f32[6,20,2]{2,1,0:T(8,128)S(1)}, u32[]{:S(2)}, u32[]{:S(2)}) collective-permute-start(f32[6,20,2]{2,1,0:T(8,128)S(1)} %get-tuple-element.72), channel_id=1, source_target_pairs={{1,0},{2,1},{3,2},{4,3},{5,4},{6,5},{7,6},{0,7},{9,8},{10,9},{11,1... | collective-permute-start | bytes 2888 | tf_op jit(solution)/shard_map/ppermute | solution.py:35
  15.3 0.7 copy-done.9
  15.9 1.3 %collective-permute-done.3 = f32[6,20,2]{2,1,0:T(8,128)S(1)} collective-permute-done((f32[6,20,2]{2,1,0:T(8,128)S(1)}, f32[6,20,2]{2,1,0:T(8,128)S(1)}, u32[]{:S(2)}, u32[]{:S(2)}) %collective-permute-start.3) | collective-permute-done | bytes 992 | tf_op jit(solution)/shard_map/ppermute | solution.py:35
  17.2 5.1 %collective-permute-done.2 = f32[6,20,2]{2,1,0:T(8,128)S(1)} collective-permute-done((f32[6,20,2]{2,1,0:T(8,128)S(1)}, f32[6,20,2]{2,1,0:T(8,128)S(1)}, u32[]{:S(2)}, u32[]{:S(2)}) %collective-permute-start.2) | collective-permute-done | bytes 992 | tf_op jit(solution)/shard_map/ppermute | solution.py:34
  22.3 0.2 fusion.4
  22.4 0.1 add_multiply_fusion.14
  22.9 0.6 copy-done.4
  23.6 0.5 collective-permute-start.4
  24.1 0.8 bitcast_select_fusion
  24.9 1.8 %collective-permute-done.4 = f32[6,2,128]{2,1,0:T(2,128)S(1)} collective-permute-done((f32[6,2,128]{2,1,0:T(2,128)S(1)}, f32[6,2,128]{2,1,0:T(2,128)S(1)}, u32[]{:S(2)}, u32[]{:S(2)}) %collective-permute-start.4) | collective-permute-done | bytes 6176 | tf_op jit(solution)/shard_map/ppermute | solution.py:34
  26.9 2.0 %collective-permute-start.6 = (f32[6,20,2]{2,1,0:T(8,128)S(1)}, f32[6,20,2]{2,1,0:T(8,128)S(1)}, u32[]{:S(2)}, u32[]{:S(2)}) collective-permute-start(f32[6,20,2]{2,1,0:T(8,128)S(1)} %get-tuple-element.69), channel_id=1, source_target_pairs={{0,1},{1,2},{2,3},{3,4},{4,5},{5,6},{6,7},{7,0},{8,9},{9,10},{10,1... | collective-permute-start | bytes 2888 | tf_op jit(solution)/shard_map/ppermute | solution.py:34
  29.0 2.2 %collective-permute-done.7 = f32[6,20,2]{2,1,0:T(8,128)S(1)} collective-permute-done((f32[6,20,2]{2,1,0:T(8,128)S(1)}, f32[6,20,2]{2,1,0:T(8,128)S(1)}, u32[]{:S(2)}, u32[]{:S(2)}) %collective-permute-start.7) | collective-permute-done | bytes 992 | tf_op jit(solution)/shard_map/ppermute | solution.py:35
  31.2 2.8 %collective-permute-done.6 = f32[6,20,2]{2,1,0:T(8,128)S(1)} collective-permute-done((f32[6,20,2]{2,1,0:T(8,128)S(1)}, f32[6,20,2]{2,1,0:T(8,128)S(1)}, u32[]{:S(2)}, u32[]{:S(2)}) %collective-permute-start.6) | collective-permute-done | bytes 992 | tf_op jit(solution)/shard_map/ppermute | solution.py:34
  34.0 0.2 fusion.9
  34.2 0.1 add_multiply_fusion.13
  34.7 0.5 collective-permute-start.8
  35.2 36.8 %all-reduce = (f32[16]{0:T(128)S(1)}, f32[16]{0:T(128)S(1)}) all-reduce(f32[16]{0:T(128)S(1)} %broadcast_multiply_fusion.1, f32[16]{0:T(128)S(1)} %get-tuple-element.8), channel_id=1, replica_groups=mesh['lat'=4,'lon'=8] {'lat','lon'}, use_global_device_ids=true, to_apply=%region_6.7 | all-reduce | flops 32 | bytes 256 | tf_op jit(solution)/shard_map/psum | solution.py:183
  72.1 4.0 %collective-permute-start.11 = (f32[6,20,2]{2,1,0:T(8,128)S(1)}, f32[6,20,2]{2,1,0:T(8,128)S(1)}, u32[]{:S(2)}, u32[]{:S(2)}) collective-permute-start(f32[6,20,2]{2,1,0:T(8,128)S(1)} %get-tuple-element.68), channel_id=1, source_target_pairs={{1,0},{2,1},{3,2},{4,3},{5,4},{6,5},{7,6},{0,7},{9,8},{10,9},{11,1... | collective-permute-start | bytes 2888 | tf_op jit(solution)/shard_map/ppermute | solution.py:35
  76.1 0.6 dynamic-slice_divide_fusion
  76.7 1.4 %collective-permute-done.11 = f32[6,20,2]{2,1,0:T(8,128)S(1)} collective-permute-done((f32[6,20,2]{2,1,0:T(8,128)S(1)}, f32[6,20,2]{2,1,0:T(8,128)S(1)}, u32[]{:S(2)}, u32[]{:S(2)}) %collective-permute-start.11) | collective-permute-done | bytes 992 | tf_op jit(solution)/shard_map/ppermute | solution.py:35
  78.1 5.1 %collective-permute-done.10 = f32[6,20,2]{2,1,0:T(8,128)S(1)} collective-permute-done((f32[6,20,2]{2,1,0:T(8,128)S(1)}, f32[6,20,2]{2,1,0:T(8,128)S(1)}, u32[]{:S(2)}, u32[]{:S(2)}) %collective-permute-start.10) | collective-permute-done | bytes 992 | tf_op jit(solution)/shard_map/ppermute | solution.py:34
  83.2 0.2 fusion.14
  83.6 0.6 fusion.88
  84.3 0.7 pad_maximum_fusion.9
  (69 shorter events, 1.9 us)
Async XLA Ops:
  1.3 1.1 %copy-start = (f32[16,35,128]{2,0,1:T(8,128)S(1)}, f32[16,35,128]{2,0,1:T(8,128)}, u32[]{:S(2)}) copy-start(f32[16,35,128]{2,0,1:T(8,128)} %param.12) | copy-start | bytes 860164
  1.3 1.1 %copy-start.1 = (f32[16,5,128]{2,0,1:T(8,128)S(1)}, f32[16,5,128]{2,0,1:T(8,128)}, u32[]{:S(2)}) copy-start(f32[16,5,128]{2,0,1:T(8,128)} %param.13) | copy-start | bytes 122884
  2.4 0.8 copy-start.7
  2.5 0.8 copy-start.8
  2.5 0.7 copy-start.6
  3.3 1.0 %copy-start.3 = (f32[3,16,128]{2,1,0:T(8,128)S(1)}, f32[3,16,128]{2,1,0:T(8,128)}, u32[]{:S(2)}) copy-start(f32[3,16,128]{2,1,0:T(8,128)} %param.18) | copy-start | bytes 73732
  4.3 0.7 copy-start.2
  5.0 3.8 %collective-permute-start.1 = (f32[6,2,128]{2,1,0:T(2,128)S(1)}, f32[6,2,128]{2,1,0:T(2,128)S(1)}, u32[]{:S(2)}, u32[]{:S(2)}) collective-permute-start(f32[6,2,128]{2,1,0:T(2,128)S(1)} %get-tuple-element.78), channel_id=1, source_target_pairs={{8,0},{16,8},{24,16},{0,24},{9,1},{17,9},{25,17},{1,25},{10,2},{18... | collective-permute-start | bytes 18440 | tf_op jit(solution)/shard_map/ppermute | solution.py:35
  7.5 3.1 %collective-permute-start = (f32[6,2,128]{2,1,0:T(2,128)S(1)}, f32[6,2,128]{2,1,0:T(2,128)S(1)}, u32[]{:S(2)}, u32[]{:S(2)}) collective-permute-start(f32[6,2,128]{2,1,0:T(2,128)S(1)} %get-tuple-element.77), channel_id=1, source_target_pairs={{0,8},{8,16},{16,24},{24,0},{1,9},{9,17},{17,25},{25,1},{2,10},{10... | collective-permute-start | bytes 18440 | tf_op jit(solution)/shard_map/ppermute | solution.py:34
  10.6 6.6 %collective-permute-start.3 = (f32[6,20,2]{2,1,0:T(8,128)S(1)}, f32[6,20,2]{2,1,0:T(8,128)S(1)}, u32[]{:S(2)}, u32[]{:S(2)}) collective-permute-start(f32[6,20,2]{2,1,0:T(8,128)S(1)} %get-tuple-element.72), channel_id=1, source_target_pairs={{1,0},{2,1},{3,2},{4,3},{5,4},{6,5},{7,6},{0,7},{9,8},{10,9},{11,1... | collective-permute-start | bytes 2888 | tf_op jit(solution)/shard_map/ppermute | solution.py:35
  15.2 7.0 %collective-permute-start.2 = (f32[6,20,2]{2,1,0:T(8,128)S(1)}, f32[6,20,2]{2,1,0:T(8,128)S(1)}, u32[]{:S(2)}, u32[]{:S(2)}) collective-permute-start(f32[6,20,2]{2,1,0:T(8,128)S(1)} %get-tuple-element.71), channel_id=1, source_target_pairs={{0,1},{1,2},{2,3},{3,4},{4,5},{5,6},{6,7},{7,0},{8,9},{9,10},{10,1... | collective-permute-start | bytes 2888 | tf_op jit(solution)/shard_map/ppermute | solution.py:34
  15.2 0.7 copy-start.9
  22.8 0.7 copy-start.4
  22.8 0.7 copy-start.5
  23.5 1.4 %collective-permute-start.5 = (f32[6,2,128]{2,1,0:T(2,128)S(1)}, f32[6,2,128]{2,1,0:T(2,128)S(1)}, u32[]{:S(2)}, u32[]{:S(2)}) collective-permute-start(f32[6,2,128]{2,1,0:T(2,128)S(1)} %get-tuple-element.76), channel_id=1, source_target_pairs={{8,0},{16,8},{24,16},{0,24},{9,1},{17,9},{25,17},{1,25},{10,2},{18... | collective-permute-start | bytes 18440 | tf_op jit(solution)/shard_map/ppermute | solution.py:35
  23.6 3.1 %collective-permute-start.4 = (f32[6,2,128]{2,1,0:T(2,128)S(1)}, f32[6,2,128]{2,1,0:T(2,128)S(1)}, u32[]{:S(2)}, u32[]{:S(2)}) collective-permute-start(f32[6,2,128]{2,1,0:T(2,128)S(1)} %get-tuple-element.75), channel_id=1, source_target_pairs={{0,8},{8,16},{16,24},{24,0},{1,9},{9,17},{17,25},{25,1},{2,10},{10... | collective-permute-start | bytes 18440 | tf_op jit(solution)/shard_map/ppermute | solution.py:34
  26.8 4.4 %collective-permute-start.7 = (f32[6,20,2]{2,1,0:T(8,128)S(1)}, f32[6,20,2]{2,1,0:T(8,128)S(1)}, u32[]{:S(2)}, u32[]{:S(2)}) collective-permute-start(f32[6,20,2]{2,1,0:T(8,128)S(1)} %get-tuple-element.70), channel_id=1, source_target_pairs={{1,0},{2,1},{3,2},{4,3},{5,4},{6,5},{7,6},{0,7},{9,8},{10,9},{11,1... | collective-permute-start | bytes 2888 | tf_op jit(solution)/shard_map/ppermute | solution.py:35
  26.9 2.0 %copy-start.10 = (s32[16]{0:T(128)S(1)}, s32[16]{0:T(128)}, u32[]{:S(2)}) copy-start(s32[16]{0:T(128)} %param.23) | copy-start | bytes 196
  26.9 7.1 %collective-permute-start.6 = (f32[6,20,2]{2,1,0:T(8,128)S(1)}, f32[6,20,2]{2,1,0:T(8,128)S(1)}, u32[]{:S(2)}, u32[]{:S(2)}) collective-permute-start(f32[6,20,2]{2,1,0:T(8,128)S(1)} %get-tuple-element.69), channel_id=1, source_target_pairs={{0,1},{1,2},{2,3},{3,4},{4,5},{5,6},{6,7},{7,0},{8,9},{9,10},{10,1... | collective-permute-start | bytes 2888 | tf_op jit(solution)/shard_map/ppermute | solution.py:34
  34.6 37.3 %collective-permute-start.9 = (f32[6,2,128]{2,1,0:T(2,128)S(1)}, f32[6,2,128]{2,1,0:T(2,128)S(1)}, u32[]{:S(2)}, u32[]{:S(2)}) collective-permute-start(f32[6,2,128]{2,1,0:T(2,128)S(1)} %get-tuple-element.74), channel_id=1, source_target_pairs={{8,0},{16,8},{24,16},{0,24},{9,1},{17,9},{25,17},{1,25},{10,2},{18... | collective-permute-start | bytes 18440 | tf_op jit(solution)/shard_map/ppermute | solution.py:35
  34.7 37.3 %collective-permute-start.8 = (f32[6,2,128]{2,1,0:T(2,128)S(1)}, f32[6,2,128]{2,1,0:T(2,128)S(1)}, u32[]{:S(2)}, u32[]{:S(2)}) collective-permute-start(f32[6,2,128]{2,1,0:T(2,128)S(1)} %get-tuple-element.73), channel_id=1, source_target_pairs={{0,8},{8,16},{16,24},{24,0},{1,9},{9,17},{17,25},{25,1},{2,10},{10... | collective-permute-start | bytes 18440 | tf_op jit(solution)/shard_map/ppermute | solution.py:34
  72.1 6.0 %collective-permute-start.11 = (f32[6,20,2]{2,1,0:T(8,128)S(1)}, f32[6,20,2]{2,1,0:T(8,128)S(1)}, u32[]{:S(2)}, u32[]{:S(2)}) collective-permute-start(f32[6,20,2]{2,1,0:T(8,128)S(1)} %get-tuple-element.68), channel_id=1, source_target_pairs={{1,0},{2,1},{3,2},{4,3},{5,4},{6,5},{7,6},{0,7},{9,8},{10,9},{11,1... | collective-permute-start | bytes 2888 | tf_op jit(solution)/shard_map/ppermute | solution.py:35
  76.1 7.0 %collective-permute-start.10 = (f32[6,20,2]{2,1,0:T(8,128)S(1)}, f32[6,20,2]{2,1,0:T(8,128)S(1)}, u32[]{:S(2)}, u32[]{:S(2)}) collective-permute-start(f32[6,20,2]{2,1,0:T(8,128)S(1)} %get-tuple-element.67), channel_id=1, source_target_pairs={{0,1},{1,2},{2,3},{3,4},{4,5},{5,6},{6,7},{7,0},{8,9},{9,10},{10,1... | collective-permute-start | bytes 2888 | tf_op jit(solution)/shard_map/ppermute | solution.py:34
where the time goes:
time: 85.7 us; the launch traced here: 85 us
  blocking collectives  36.8 us (43%)
  waiting for transfers between devices  22.4 us (26%)
  starting transfers between devices  14.3 us (17%)
  other arithmetic  7.53 us (9%)
  local copies, waits for them, and re-layouts  3.03 us (4%)
  between operations  0.96 us (1%)
    psum x1, blocking collectives, local(): whole_sum, whole_cells = lax.psum((part_sum, part_cells), ('lat', 'lon'))  36.8 us
    ppermute x6, waiting for transfers between devices, with_halo(): before = lax.ppermute(last, axis, up)  16.4 us
    ppermute x6, starting transfers between devices, with_halo(): after = lax.ppermute(leading, axis, down)  11.3 us
    ppermute x6, waiting for transfers between devices, with_halo(): after = lax.ppermute(leading, axis, down)  6.01 us
    ppermute x6, starting transfers between devices, with_halo(): before = lax.ppermute(last, axis, up)  3 us
    unnamed x24, local copies, waits for them, and re-layouts  2.73 us
  transfers between devices with their start and end apart: 12, of which 9 were waited for; matrix products, arithmetic and copies ran while one was open for 2% of the time, Pallas kernels for 0%

commit v1 on v0

v1 whole, which is shorter than its diff:
```python
import functools

import jax
import jax.numpy as jnp
from jax import lax
from jax.experimental import pallas as pl
from jax.experimental.pallas import tpu as pltpu
from jax.sharding import PartitionSpec as P

DEPTH_CLASSES = 5
VERTICAL_LEVELS = 7
SUBCYCLES = 3
SWEEPS = 2
BANDS_DEV = 4

FREEZE_POINT = -1.8
BASE_CONDUCT = 2.03
SALT_CONDUCT = 0.416
GROWTH_RATE = 0.02
STRENGTH_DECAY = 5.0
ELLIPSE_SQUARE = 4.0
STRAIN_FLOOR = 0.0025
STRESS_RELAX = 0.5
MOMENTUM_STEP = 0.5
WATER_DRAG = 1.0

HALO = 2 * SUBCYCLES
EDGE = 8
FIELDS = 10
EARLY_CLASSES = 1

MESH = pl.DeviceIdType.MESH


def step_columns(temps, depth, surface, seawater):
    inverse = 1.0 / depth
    scaled = inverse * inverse
    half = 0.5 * scaled
    guess = temps
    for turn in range(SWEEPS):
        conduct = [BASE_CONDUCT + SALT_CONDUCT / g for g in guess]
        coupling = [scaled * conduct[0]]
        for k in range(1, VERTICAL_LEVELS):
            coupling.append(half * (conduct[k - 1] + conduct[k]))
        coupling.append(scaled * conduct[-1])
        ratio, done = [], []
        for k in range(VERTICAL_LEVELS):
            source = temps[k]
            divisor = 1.0 + coupling[k] + coupling[k + 1]
            if k == 0:
                source = source + coupling[0] * surface
            else:
                divisor = divisor - coupling[k] * ratio[k - 1]
                source = source + coupling[k] * done[k - 1]
            if k == VERTICAL_LEVELS - 1:
                source = source + coupling[k + 1] * FREEZE_POINT
            scale = 1.0 / divisor
            if k < VERTICAL_LEVELS - 1:
                ratio.append(coupling[k + 1] * scale)
            done.append(source * scale)
        solved = list(done)
        for k in range(VERTICAL_LEVELS - 2, -1, -1):
            solved[k] = done[k] + ratio[k] * solved[k + 1]
        guess = solved
    bottom = guess[-1]
    thick = (
        depth
        + GROWTH_RATE * (BASE_CONDUCT + SALT_CONDUCT / bottom) * (FREEZE_POINT - bottom) * inverse
        - seawater
    )
    return guess, thick


def subcycle(u, v, s1, s2, s12, strength, keep, push_scale, force_x, force_y):
    rows, cols = u.shape

    def dx(f):
        return pltpu.roll(f, cols - 1, 1) - pltpu.roll(f, 1, 1)

    def dy(f):
        return pltpu.roll(f, rows - 1, 0) - pltpu.roll(f, 1, 0)

    ux, vy, uy, vx = dx(u), dy(v), dy(u), dx(v)
    divergence = 0.5 * (ux + vy)
    tension = 0.5 * (ux - vy)
    shearing = 0.5 * (uy + vx)
    deformation = jnp.sqrt(
        divergence * divergence
        + (tension * tension + shearing * shearing) * (1.0 / ELLIPSE_SQUARE)
        + STRAIN_FLOOR
    )
    relax = 1.0 / (1.0 + STRESS_RELAX)
    viscous = (STRESS_RELAX * relax) * strength / deformation
    s1 = relax * s1 + viscous * (divergence - deformation)
    s2 = relax * s2 + viscous * tension * (1.0 / ELLIPSE_SQUARE)
    s12 = relax * s12 + viscous * shearing * (0.5 / ELLIPSE_SQUARE)
    push_x = dx(0.5 * (s1 + s2)) + dy(s12)
    push_y = dx(s12) + dy(0.5 * (s1 - s2))
    u = keep * u + push_scale * push_x + force_x
    v = keep * v + push_scale * push_y + force_y
    return u, v, s1, s2, s12


def as_column(row, rows):
    shape = (rows, rows)
    pick = lax.broadcasted_iota(jnp.int32, shape, 0) == lax.broadcasted_iota(jnp.int32, shape, 1)
    wide = jnp.broadcast_to(row.astype(jnp.float32), shape)
    return jnp.sum(jnp.where(pick, wide, 0.0), axis=1, keepdims=True)


def kernel(n_lat, n_lon, *refs):
    inputs, outputs, scratch = refs[:12], refs[12:17], refs[17:]
    temp_out, thick_out, vel_out, stress_out, zonal_out = outputs
    held = scratch[:12]
    (own, packed, from_up, from_down, from_west, from_east, lat_parts, lon_parts) = scratch[12:20]
    (in_sem, halo_send, halo_recv, lat_send, lat_recv, lon_send, lon_recv) = scratch[20:]
    (temp_in, depth_in, area_in, surf_in, sea_in, vel_in, stress_in) = held[:7]
    (wind_in, current_in, land_in, ice_in, band_in) = held[7:]
    rows, cols = surf_in.shape
    lat, lon = lax.axis_index("lat"), lax.axis_index("lon")
    lats = [lax.rem(lat + d, n_lat) for d in range(n_lat)]
    lons = [lax.rem(lon + d, n_lon) for d in range(n_lon)]
    south, north, east, west = lats[1], lats[-1], lons[1], lons[-1]

    order = (1, 2, 5, 6, 7, 8, 9, 0, 3, 4, 10, 11)
    loads = [pltpu.make_async_copy(inputs[i], held[i], in_sem.at[i]) for i in range(12)]
    for i in order:
        loads[i].start()

    barrier = pltpu.get_barrier_semaphore()
    partners = [(lat, g) for g in lons[1:]] + [(a, lon) for a in lats[1:]]
    partners += [(a, g) for a in (north, south) for g in (west, east)]
    for partner in partners:
        pl.semaphore_signal(barrier, inc=1, device_id=partner, device_id_type=MESH)

    for i in (1, 2, 5, 6, 7, 8, 9):
        loads[i].wait()
    volume = area_in[:, 0, :] * depth_in[:, 0, :]
    coverage = area_in[:, 0, :]
    for c in range(1, DEPTH_CLASSES):
        volume = volume + area_in[:, c, :] * depth_in[:, c, :]
        coverage = coverage + area_in[:, c, :]
    strength = volume * jnp.exp(-STRENGTH_DECAY * (1.0 - coverage))
    drag = 1.0 / (1.0 + MOMENTUM_STEP * WATER_DRAG)
    keep = land_in[...].astype(jnp.float32) * drag
    forced = MOMENTUM_STEP * keep
    push_scale = 0.5 * forced / (1.0 + volume)
    fields = [vel_in[0], vel_in[1], stress_in[0], stress_in[1], stress_in[2], strength, keep]
    fields += [push_scale]
    fields += [forced * (wind_in[i] + WATER_DRAG * current_in[i]) for i in range(2)]
    lane = lax.broadcasted_iota(jnp.int32, (rows, cols), 1)
    pack = jnp.zeros((rows, cols), jnp.float32)
    for f in range(FIELDS):
        first = 2 * HALO * f
        turned = pltpu.roll(fields[f], (first + HALO) % cols, 1)
        pack = jnp.where((lane >= first) & (lane < first + 2 * HALO), turned, pack)
    packed[...] = pack
    for f in range(FIELDS):
        own[f] = fields[f]

    for i in (0, 3, 4, 10, 11):
        loads[i].wait()
    surface, seawater = surf_in[...], sea_in[...]
    icy = as_column(ice_in[...], rows) == 1.0

    def thermo(c):
        first = c * VERTICAL_LEVELS
        temps = [temp_in[:, first + k, :] for k in range(VERTICAL_LEVELS)]
        depth = depth_in[:, c, :]
        stepped, thick = step_columns(temps, depth, surface, seawater)
        thick = jnp.where(icy, thick, depth)
        for k in range(VERTICAL_LEVELS):
            temp_out[:, first + k, :] = jnp.where(icy, stepped[k], temps[k])
        thick_out[:, c, :] = thick
        return area_in[:, c, :] * thick

    after = jnp.zeros((rows, cols), jnp.float32)
    for c in range(EARLY_CLASSES):
        after = after + thermo(c)

    pl.semaphore_wait(barrier, len(partners))

    tail, head = pl.ds(rows - EDGE, EDGE), pl.ds(0, EDGE)
    above, middle, below = pl.ds(0, EDGE), pl.ds(EDGE, rows), pl.ds(EDGE + rows, EDGE)
    plan = (
        (packed.at[tail], from_west.at[above], (south, east)),
        (packed.at[tail], from_east.at[above], (south, west)),
        (packed.at[head], from_west.at[below], (north, east)),
        (packed.at[head], from_east.at[below], (north, west)),
        (packed, from_west.at[middle], (lat, east)),
        (packed, from_east.at[middle], (lat, west)),
        (own.at[:, tail], from_up, (south, lon)),
        (own.at[:, head], from_down, (north, lon)),
    )
    halos = [
        pltpu.make_async_remote_copy(
            src_ref=source,
            dst_ref=target,
            send_sem=halo_send.at[i],
            recv_sem=halo_recv.at[i],
            device_id=device,
            device_id_type=MESH,
        )
        for i, (source, target, device) in enumerate(plan)
    ]
    for copy in halos:
        copy.start()

    for c in range(EARLY_CLASSES, DEPTH_CLASSES):
        after = after + thermo(c)
    total = jnp.sum(after, axis=1, keepdims=True)
    width = lat_parts.shape[-1]
    member = as_column(band_in[...], rows).astype(jnp.int32) == lax.broadcasted_iota(
        jnp.int32, (rows, width), 1
    )
    sums = jnp.sum(jnp.where(member, total, 0.0), axis=0, keepdims=True)
    cells = jnp.sum(jnp.where(member, float(cols), 0.0), axis=0, keepdims=True)
    top = lax.broadcasted_iota(jnp.int32, (EDGE, width), 0) == 0
    lat_parts[lat] = jnp.where(top, sums, cells)

    def share(parts, here, send_sem, recv_sem, devices):
        copies = [
            pltpu.make_async_remote_copy(
                src_ref=parts.at[here],
                dst_ref=parts.at[here],
                send_sem=send_sem.at[d],
                recv_sem=recv_sem.at[d],
                device_id=device,
                device_id_type=MESH,
            )
            for d, device in enumerate(devices)
        ]
        for copy in copies:
            copy.start()
        return copies

    lat_copies = share(lat_parts, lat, lat_send, lat_recv, [(a, lon) for a in lats[1:]])
    for copy in lat_copies:
        copy.wait_recv()
    lon_parts[lon] = jnp.sum(lat_parts[...], axis=0)
    lon_copies = share(lon_parts, lon, lon_send, lon_recv, [(lat, g) for g in lons[1:]])

    for copy in halos:
        copy.wait_recv()
    tall = rows + 2 * EDGE
    place = lax.broadcasted_iota(jnp.int32, (tall, cols), 1)
    merged = jnp.where(lax.rem(place, 2 * HALO) < HALO, from_west[...], from_east[...])
    low = jnp.where(lat == 0, EDGE, 0)
    high = jnp.where(lat == n_lat - 1, EDGE + rows, tall)
    row_id = lax.broadcasted_iota(jnp.int32, (tall, 2 * cols), 0)
    inside = (row_id >= low) & (row_id < high)
    state = []
    for f in range(FIELDS):
        centre = jnp.concatenate([from_up[f], own[f], from_down[f]], axis=0)
        sides = pltpu.roll(merged, (cols - 2 * HALO * f - HALO) % cols, 1)
        state.append(jnp.where(inside, jnp.concatenate([centre, sides], axis=1), 0.0))
    moving, fixed = state[:5], state[5:]
    for turn in range(SUBCYCLES):
        moving = subcycle(*moving, *fixed)
    for i in range(2):
        vel_out[i] = moving[i][EDGE : EDGE + rows, :cols]
    for i in range(3):
        stress_out[i] = moving[2 + i][EDGE : EDGE + rows, :cols]

    for copy in lon_copies:
        copy.wait_recv()
    zonal_out[...] = jnp.sum(lon_parts[...], axis=0)
    for copy in halos + lat_copies + lon_copies:
        copy.wait_send()


def local(n_lat, n_lon, *args):
    args = list(args)
    args[11] = args[11].reshape(1, -1)
    rows, cols = args[3].shape
    bands = BANDS_DEV * n_lat
    width = -(-bands // cols) * cols
    tall = rows + 2 * EDGE
    f32 = jnp.float32
    vmem = pl.BlockSpec(memory_space=pltpu.VMEM)
    outs = [jax.ShapeDtypeStruct(args[i].shape, f32) for i in (0, 1, 5, 6)]
    outs.append(jax.ShapeDtypeStruct((EDGE, width), f32))
    dma = pltpu.SemaphoreType.DMA
    temp, thick, vel, stress, zonal = pl.pallas_call(
        functools.partial(kernel, n_lat, n_lon),
        out_shape=outs,
        in_specs=[pl.BlockSpec(memory_space=pl.ANY)] * 12,
        out_specs=[vmem] * 5,
        scratch_shapes=[pltpu.VMEM(a.shape, a.dtype) for a in args]
        + [
            pltpu.VMEM((FIELDS, rows, cols), f32),
            pltpu.VMEM((rows, cols), f32),
            pltpu.VMEM((FIELDS, EDGE, cols), f32),
            pltpu.VMEM((FIELDS, EDGE, cols), f32),
            pltpu.VMEM((tall, cols), f32),
            pltpu.VMEM((tall, cols), f32),
            pltpu.VMEM((n_lat, EDGE, width), f32),
            pltpu.VMEM((n_lon, EDGE, width), f32),
            dma((12,)),
            dma((8,)),
            dma((8,)),
            dma((n_lat - 1,)),
            dma((n_lat - 1,)),
            dma((n_lon - 1,)),
            dma((n_lon - 1,)),
        ],
        compiler_params=pltpu.CompilerParams(collective_id=0, has_side_effects=True),
        name="ice_step",
    )(*args)
    start = lax.axis_index("lat") * BANDS_DEV
    mine = lax.dynamic_slice_in_dim(zonal, start, BANDS_DEV, axis=1)
    return (temp, thick, vel, stress, mine[0] / mine[1])


def solution(mesh):
    shape = dict(mesh.shape)
    return jax.shard_map(
        functools.partial(local, shape["lat"], shape["lon"]),
        mesh=mesh,
        in_specs=(
            P("lat", None, "lon"),
            P("lat", None, "lon"),
            P("lat", None, "lon"),
            P("lat", "lon"),
            P("lat", "lon"),
            P(None, "lat", "lon"),
            P(None, "lat", "lon"),
            P(None, "lat", "lon"),
            P(None, "lat", "lon"),
            P("lat", "lon"),
            P("lon", "lat"),
            P("lat"),
        ),
        out_specs=(
            P("lat", None, "lon"),
            P("lat", None, "lon"),
            P(None, "lat", "lon"),
            P(None, "lat", "lon"),
            P("lat"),
        ),
        check_vma=False,
    )
```

time: 85.7 us -> 24.3 us (0.28)
  blocking collectives: 36.8 us -> 0 us
  waiting for transfers between devices: 22.4 us -> 0 us
  Pallas kernels: 0 us -> 15.2 us
  starting transfers between devices: 14.3 us -> 0 us
  other arithmetic: 7.53 us -> 0.52 us
  local copies, waits for them, and re-layouts: 3.03 us -> 7.6 us
    psum x1 -> x0, blocking collectives: 36.8 us -> none  [local(): whole_sum, whole_cells = lax.psum((part_sum, part_cells), ('lat', 'lon'))]
    ppermute x12 -> x0, waiting for transfers between devices: 22.4 us -> none  [the longest x6 16.4 us: with_halo(): before = lax.ppermute(last, axis, up)]
    pallas_call x0 -> x1, Pallas kernels: none -> 15.2 us  [local(): pl.pallas_call(functools.partial(kernel, n_lat, n_lon), out_shape=outs, i...]
    ppermute x12 -> x0, starting transfers between devices: 14.3 us -> none  [the longest x6 11.3 us: with_halo(): after = lax.ppermute(leading, axis, down)]
    unnamed x24 -> x19, local copies, waits for them, and re-layouts: 2.73 us -> 7.53 us
    div x8 -> x1, other arithmetic: 2.61 us -> 0.52 us  [local(): return (temp, thick, vel, stress, mine[0] / mine[1])]
    select_n x4 -> x0, other arithmetic: 1.27 us -> none  [the longest x1 0.8 us: local(): temp_after = jnp.where(strip_ice, stepped_temp, layer_temp)]
    another operation x7 -> x0, other arithmetic: 1.11 us -> none  [the longest x3 0.85 us: stress_update(): return jnp.stack([bulk_new, tension_new, shear_new])]
  transfers between devices with their start and end apart: 12 -> 0, of which waited for: 9 -> 0; matrix products, arithmetic and copies ran while one was open for 2% -> 0% of each run, Pallas kernels for 0% -> 0%
where the time goes in v1:
time: 24.3 us; the launch traced here: 24 us
  Pallas kernels  15.2 us (63%)
  local copies, waits for them, and re-layouts  7.6 us (31%)
  between operations  0.66 us (3%)
  other arithmetic  0.52 us (2%)
    pallas_call x1, Pallas kernels, local(): pl.pallas_call(functools.partial(kernel, n_lat, n_lon), out_shape=outs, i...  15.2 us
    unnamed x19, local copies, waits for them, and re-layouts  7.53 us
    div x1, other arithmetic, local(): return (temp, thick, vel, stress, mine[0] / mine[1])  0.52 us

profile of v1, /device:TPU:0, one launch (start us, length us, event | category | flops | bytes accessed | tf_op | source)
XLA Modules:
  0.0 24.0 jit_solution(12734123703077721590)
XLA Ops:
  0.6 0.0 copy-start.1
  0.6 1.8 %copy.17.refs_0_ = f32[16,35,128]{2,1,0:T(8,128)} copy(f32[16,35,128]{2,0,1:T(8,128)} %param.12) | data formatting | bytes 573440 | tf_op args[0]
  2.4 0.0 copy-done.1
  2.4 0.0 copy-start.2
  2.4 0.6 %copy.18.refs_1_ = f32[16,5,128]{2,1,0:T(8,128)} copy(f32[16,5,128]{2,0,1:T(8,128)S(1)} %copy-done.1) | data formatting | bytes 81920 | tf_op args[1]
  3.1 0.1 copy-done.2
  3.2 0.6 %copy.19.refs_2_ = f32[16,5,128]{2,1,0:T(8,128)} copy(f32[16,5,128]{2,0,1:T(8,128)S(1)} %copy-done.2) | data formatting | bytes 81920 | tf_op args[2]
  3.9 15.2 %ice_step.1 = (f32[16,35,128]{2,1,0:T(8,128)}, f32[16,5,128]{2,1,0:T(8,128)}, f32[2,16,128]{2,1,0:T(8,128)}, f32[3,16,128]{2,1,0:T(8,128)}, f32[8,128]{1,0:T(8,128)}) custom-call(f32[16,35,128]{2,1,0:T(8,128)} %copy.17.refs_0_, f32[16,5,128]{2,1,0:T(8,128)} %copy.18.refs_1_, f32[16,5,128]{2,1,0:T(8,128)} %copy.19.refs_2_, f32[16,128]{1,0:T(8,128)} %refs_3_.1, ...), custom_call_target="tpu_custom_call" | custom-call | tf_op jit(solution)/shard_map/ice_step/pallas_call | solution.py:284
  19.1 0.0 copy-start
  19.1 1.8 %copy.20 = f32[16,35,128]{2,0,1:T(8,128)} copy(f32[16,35,128]{2,1,0:T(8,128)} %get-tuple-element.15) | data formatting | bytes 573440
  20.9 0.0 copy-done
  20.9 0.6 %copy.21 = f32[16,5,128]{2,0,1:T(8,128)} copy(f32[16,5,128]{2,1,0:T(8,128)S(1)} %copy-done) | data formatting | bytes 81920
  21.5 0.0 copy-start.4
  21.5 0.0 copy-start.5
  21.5 0.0 copy-start.3
  21.5 0.7 %copy-done.5 = f32[8,128]{1,0:T(8,128)S(1)} copy-done((f32[8,128]{1,0:T(8,128)S(1)}, f32[8,128]{1,0:T(8,128)}, u32[]{:S(2)}) %copy-start.5) | copy-done | bytes 4120
  22.2 0.1 constant_dynamic-slice_fusion
  22.3 0.5 %fusion = f32[4]{0:T(128)} fusion(f32[8,4]{1,0:T(8,128)S(1)} %constant_dynamic-slice_fusion), kind=kLoop, calls=%fused_computation.1 | loop fusion | flops 4 | bytes 48 | tf_op jit(solution)/shard_map/div | solution.py:312
  22.8 0.0 copy-done.4
  22.8 0.6 %copy.24 = f32[2,16,128]{2,1,0:T(8,128)} copy(f32[2,16,128]{2,1,0:T(8,128)S(1)} %copy-done.4) | data formatting | bytes 32768
  23.4 0.0 copy-done.3
  23.4 0.6 %copy.25 = f32[3,16,128]{2,1,0:T(8,128)} copy(f32[3,16,128]{2,1,0:T(8,128)S(1)} %copy-done.3) | data formatting | bytes 49152
Async XLA Ops:
  0.6 1.8 %copy-start.1 = (f32[16,5,128]{2,0,1:T(8,128)S(1)}, f32[16,5,128]{2,0,1:T(8,128)}, u32[]{:S(2)}) copy-start(f32[16,5,128]{2,0,1:T(8,128)} %param.13) | copy-start | bytes 122884
  2.4 0.8 %copy-start.2 = (f32[16,5,128]{2,0,1:T(8,128)S(1)}, f32[16,5,128]{2,0,1:T(8,128)}, u32[]{:S(2)}) copy-start(f32[16,5,128]{2,0,1:T(8,128)} %param.14) | copy-start | bytes 122884
  19.1 1.8 %copy-start = (f32[16,5,128]{2,1,0:T(8,128)S(1)}, f32[16,5,128]{2,1,0:T(8,128)}, u32[]{:S(2)}) copy-start(f32[16,5,128]{2,1,0:T(8,128)} %get-tuple-element.16) | copy-start | bytes 122884
  21.5 1.3 %copy-start.4 = (f32[2,16,128]{2,1,0:T(8,128)S(1)}, f32[2,16,128]{2,1,0:T(8,128)}, u32[]{:S(2)}) copy-start(f32[2,16,128]{2,1,0:T(8,128)} %get-tuple-element.27) | copy-start | bytes 49156
  21.5 0.7 %copy-start.5 = (f32[8,128]{1,0:T(8,128)S(1)}, f32[8,128]{1,0:T(8,128)}, u32[]{:S(2)}) copy-start(f32[8,128]{1,0:T(8,128)} %get-tuple-element.14) | copy-start | bytes 12292
  21.5 1.9 %copy-start.3 = (f32[3,16,128]{2,1,0:T(8,128)S(1)}, f32[3,16,128]{2,1,0:T(8,128)}, u32[]{:S(2)}) copy-start(f32[3,16,128]{2,1,0:T(8,128)} %get-tuple-element.28) | copy-start | bytes 73732

commit v2 on v1

--- a/solution.py
+++ b/solution.py
@@ -135,11 +135,11 @@
 
     for i in (1, 2, 5, 6, 7, 8, 9):
         loads[i].wait()
-    volume = area_in[:, 0, :] * depth_in[:, 0, :]
-    coverage = area_in[:, 0, :]
+    volume = area_in[0] * depth_in[0]
+    coverage = area_in[0]
     for c in range(1, DEPTH_CLASSES):
-        volume = volume + area_in[:, c, :] * depth_in[:, c, :]
-        coverage = coverage + area_in[:, c, :]
+        volume = volume + area_in[c] * depth_in[c]
+        coverage = coverage + area_in[c]
     strength = volume * jnp.exp(-STRENGTH_DECAY * (1.0 - coverage))
     drag = 1.0 / (1.0 + MOMENTUM_STEP * WATER_DRAG)
     keep = land_in[...].astype(jnp.float32) * drag
@@ -165,14 +165,14 @@
 
     def thermo(c):
         first = c * VERTICAL_LEVELS
-        temps = [temp_in[:, first + k, :] for k in range(VERTICAL_LEVELS)]
-        depth = depth_in[:, c, :]
+        temps = [temp_in[first + k] for k in range(VERTICAL_LEVELS)]
+        depth = depth_in[c]
         stepped, thick = step_columns(temps, depth, surface, seawater)
         thick = jnp.where(icy, thick, depth)
         for k in range(VERTICAL_LEVELS):
-            temp_out[:, first + k, :] = jnp.where(icy, stepped[k], temps[k])
-        thick_out[:, c, :] = thick
-        return area_in[:, c, :] * thick
+            temp_out[first + k] = jnp.where(icy, stepped[k], temps[k])
+        thick_out[c] = thick
+        return area_in[c] * thick
 
     after = jnp.zeros((rows, cols), jnp.float32)
     for c in range(EARLY_CLASSES):
@@ -264,13 +264,28 @@
 
     for copy in lon_copies:
         copy.wait_recv()
-    zonal_out[...] = jnp.sum(lon_parts[...], axis=0)
+    whole = jnp.sum(lon_parts[...], axis=0)
+    mean = whole[:1] / jnp.maximum(whole[1:2], 1.0)
+    mine = jnp.zeros((1, BANDS_DEV), jnp.float32)
+    for a in range(n_lat):
+        mine = jnp.where(lat == a, mean[:, a * BANDS_DEV : (a + 1) * BANDS_DEV], mine)
+    zonal_out[...] = mine
     for copy in halos + lat_copies + lon_copies:
         copy.wait_send()
 
 
+def put_out(*refs):
+    sem = refs[10]
+    copies = [pltpu.make_async_copy(refs[i], refs[5 + i], sem.at[i]) for i in range(5)]
+    for copy in copies:
+        copy.start()
+    for copy in copies:
+        copy.wait()
+
+
 def local(n_lat, n_lon, *args):
     args = list(args)
+    args[:3] = [jnp.transpose(a, (1, 0, 2)) for a in args[:3]]
     args[11] = args[11].reshape(1, -1)
     rows, cols = args[3].shape
     bands = BANDS_DEV * n_lat
@@ -278,12 +293,11 @@
     tall = rows + 2 * EDGE
     f32 = jnp.float32
     vmem = pl.BlockSpec(memory_space=pltpu.VMEM)
-    outs = [jax.ShapeDtypeStruct(args[i].shape, f32) for i in (0, 1, 5, 6)]
-    outs.append(jax.ShapeDtypeStruct((EDGE, width), f32))
+    shapes = [args[i].shape for i in (0, 1, 5, 6)] + [(1, BANDS_DEV)]
     dma = pltpu.SemaphoreType.DMA
-    temp, thick, vel, stress, zonal = pl.pallas_call(
+    results = pl.pallas_call(
         functools.partial(kernel, n_lat, n_lon),
-        out_shape=outs,
+        out_shape=[pltpu.VMEM(shape, f32) for shape in shapes],
         in_specs=[pl.BlockSpec(memory_space=pl.ANY)] * 12,
         out_specs=[vmem] * 5,
         scratch_shapes=[pltpu.VMEM(a.shape, a.dtype) for a in args]
@@ -307,9 +321,16 @@
         compiler_params=pltpu.CompilerParams(collective_id=0, has_side_effects=True),
         name="ice_step",
     )(*args)
-    start = lax.axis_index("lat") * BANDS_DEV
-    mine = lax.dynamic_slice_in_dim(zonal, start, BANDS_DEV, axis=1)
-    return (temp, thick, vel, stress, mine[0] / mine[1])
+    temp, thick, vel, stress, zonal = pl.pallas_call(
+        put_out,
+        out_shape=[jax.ShapeDtypeStruct(shape, f32) for shape in shapes],
+        in_specs=[vmem] * 5,
+        out_specs=[pl.BlockSpec(memory_space=pl.ANY)] * 5,
+        scratch_shapes=[dma((5,))],
+        name="put_out",
+    )(*[pltpu.with_memory_space_constraint(r, pltpu.VMEM) for r in results])
+    temp, thick = [jnp.transpose(a, (1, 0, 2)) for a in (temp, thick)]
+    return (temp, thick, vel, stress, zonal.reshape(BANDS_DEV))
 
 
 def solution(mesh):

time: 24.3 us -> 14.8 us (0.61)
  local copies, waits for them, and re-layouts: 7.6 us -> 0 us
  Pallas kernels: 15.2 us -> 14 us
  other arithmetic: 0.52 us -> 0 us
    unnamed x19 -> x0, local copies, waits for them, and re-layouts: 7.53 us -> none
    pallas_call x1 -> x2, Pallas kernels: 15.2 us -> 14 us  [the longest x1 13.3 us: local(): pl.pallas_call(functools.partial(kernel, n_lat, n_lon), out_shape=[pltpu....]
    div x1 -> x0, other arithmetic: 0.52 us -> none  [local(): return (temp, thick, vel, stress, mine[0] / mine[1])]
where the time goes in v2:
time: 14.8 us; the launch traced here: 14.7 us
  Pallas kernels  14 us (95%)
  between operations  0.64 us (4%)
    pallas_call x1, Pallas kernels, local(): pl.pallas_call(functools.partial(kernel, n_lat, n_lon), out_shape=[pltpu....  13.3 us
    pallas_call x1, Pallas kernels, local(): pl.pallas_call(put_out, out_shape=[jax.ShapeDtypeStruct(shape, f32) for s...  0.77 us

profile of v2, /device:TPU:0, one launch (start us, length us, event | category | flops | bytes accessed | tf_op | source)
XLA Modules:
  0.0 14.7 jit_solution(3421717250890521132)
XLA Ops:
  0.6 13.3 %ice_step.1 = (f32[35,16,128]{2,1,0:T(8,128)S(1)}, f32[5,16,128]{2,1,0:T(8,128)S(1)}, f32[2,16,128]{2,1,0:T(8,128)S(1)}, f32[3,16,128]{2,1,0:T(8,128)S(1)}, f32[1,4]{1,0:T(1,128)S(1)}) custom-call(f32[35,16,128]{2,1,0:T(8,128)} %bitcast.7, f32[5,16,128]{2,1,0:T(8,128)} %bitcast.8, f32[5,16,128]{2,1,0:T(8,128)} %bitcast.9, f32[16,128]{1,0:T(8,128)} %refs_3_.1, ...), custom_call_target="tpu_custom_call" | custom-call | tf_op jit(solution)/shard_map/ice_step/pallas_call | solution.py:298
  13.9 0.8 %put_out.1 = (f32[35,16,128]{2,1,0:T(8,128)}, f32[5,16,128]{2,1,0:T(8,128)}, f32[2,16,128]{2,1,0:T(8,128)}, f32[3,16,128]{2,1,0:T(8,128)}, f32[1,4]{1,0:T(1,128)}) custom-call(f32[35,16,128]{2,1,0:T(8,128)S(1)} %get-tuple-element.15.refs_0_, f32[5,16,128]{2,1,0:T(8,128)S(1)} %get-tuple-element.16.refs_1_, f32[2,16,128]{2,1,0:T(8,128)S(1)} %get-tuple-element.17.refs_2_, ...), custom_call_target="tpu_custom_call" | custom-call | tf_op jit(solution)/shard_map/put_out/pallas_call | solution.py:324

commit v3 on v2

--- a/solution.py
+++ b/solution.py
@@ -27,7 +27,7 @@
 HALO = 2 * SUBCYCLES
 EDGE = 8
 FIELDS = 10
-EARLY_CLASSES = 1
+EARLY_CLASSES = 2
 
 MESH = pl.DeviceIdType.MESH
 

time: 14.8 us -> 14.9 us (level)
  no operation moved by 1% of the time
where the time goes in v3:
time: 14.9 us; the launch traced here: 14.7 us
  Pallas kernels  14.1 us (95%)
  between operations  0.64 us (4%)
    pallas_call x1, Pallas kernels, local(): pl.pallas_call(functools.partial(kernel, n_lat, n_lon), out_shape=[pltpu....  13.3 us
    pallas_call x1, Pallas kernels, local(): pl.pallas_call(put_out, out_shape=[jax.ShapeDtypeStruct(shape, f32) for s...  0.77 us

profile of v3, /device:TPU:0, one launch (start us, length us, event | category | flops | bytes accessed | tf_op | source)
XLA Modules:
  0.0 14.7 jit_solution(15996838669029709203)
XLA Ops:
  0.6 13.3 %ice_step.1 = (f32[35,16,128]{2,1,0:T(8,128)S(1)}, f32[5,16,128]{2,1,0:T(8,128)S(1)}, f32[2,16,128]{2,1,0:T(8,128)S(1)}, f32[3,16,128]{2,1,0:T(8,128)S(1)}, f32[1,4]{1,0:T(1,128)S(1)}) custom-call(f32[35,16,128]{2,1,0:T(8,128)} %bitcast.7, f32[5,16,128]{2,1,0:T(8,128)} %bitcast.8, f32[5,16,128]{2,1,0:T(8,128)} %bitcast.9, f32[16,128]{1,0:T(8,128)} %refs_3_.1, ...), custom_call_target="tpu_custom_call" | custom-call | tf_op jit(solution)/shard_map/ice_step/pallas_call | solution.py:298
  13.9 0.8 %put_out.1 = (f32[35,16,128]{2,1,0:T(8,128)}, f32[5,16,128]{2,1,0:T(8,128)}, f32[2,16,128]{2,1,0:T(8,128)}, f32[3,16,128]{2,1,0:T(8,128)}, f32[1,4]{1,0:T(1,128)}) custom-call(f32[35,16,128]{2,1,0:T(8,128)S(1)} %get-tuple-element.15.refs_0_, f32[5,16,128]{2,1,0:T(8,128)S(1)} %get-tuple-element.16.refs_1_, f32[2,16,128]{2,1,0:T(8,128)S(1)} %get-tuple-element.17.refs_2_, ...), custom_call_target="tpu_custom_call" | custom-call | tf_op jit(solution)/shard_map/put_out/pallas_call | solution.py:324
